TPU v7x, 256 devices: a whole 4x4x8 slice. The times are simulated.
256 devices in a mesh: dp: 4 (over x), expert: 64 (over y, z, core).
Axes of the slice: x: 4, y: 4, z: 8, core: 2. Of those that a mesh axis runs over, the one named last changes fastest.
Arguments:
- hidden: bfloat16 [4, 4096, 2, 2048], P('dp', 'expert'), may hold values from -6 to 6
- queries: bfloat16 [4, 4096, 2, 4096], P('dp', 'expert'), may hold values from -45 to 45
- latents: bfloat16 [4, 4096, 2, 512], P('dp', 'expert'), may hold values from -165 to 165
- mem_latents: bfloat16 [4, 32, 2, 512], P('dp'), may hold values from -6 to 6
- lengths: int32 [4, 2], P('dp'), may hold values from 2048 to 4096
- ids: int32 [4, 4096, 2, 6], P('dp', 'expert'), may hold values from 0 to 63, all different within a row; in each aligned block of 128 rows (0 to 127, 128 to 255, ..., all dimensions but the last counted through in order) at most 14 rows name the same one
- gates: bfloat16 [4, 4096, 2, 6], P('dp', 'expert'), may hold values from 0.049804688 to 0.5
- norm_gain: bfloat16 [2048], replicated, may hold values from 0.25 to 1.75
- w_uv: bfloat16 [8, 512, 128], P('dp'), may hold values from -0.25 to 0.25
- w_out: bfloat16 [1024, 2048], P('dp'), may hold values from -0.1875 to 0.1875
- w_gate: bfloat16 [64, 2048, 704], P('expert'), may hold values from -0.125 to 0.125
- w_up: bfloat16 [64, 2048, 704], P('expert'), may hold values from -0.125 to 0.125
- w_down: bfloat16 [64, 704, 2048], P('expert'), may hold values from -0.21875 to 0.21875
Outputs:
- layer_out: bfloat16 [4, 4096, 2, 2048], P('dp', 'expert')
Inputs may be any that keep to these rules, and one draw needn't show every extreme that they name: `ids`: each row names 6 different experts; the rows of one device (aligned blocks of 128 rows in the order of the leading dimensions) name any one expert at most 14 times, a bound that some block reaches.
All inputs are finite; a program needn't handle non-finite values.
Results may differ from a plain program's by a relative error of at most 0.007.
Values may be sent and summed in bfloat16 or wider, within the bound.
A program may use at most 128 MiB of HBM per device.

v0:
```python
import jax
import jax.numpy as jnp
from jax import lax
from jax.sharding import PartitionSpec as P

score_scale = 192.0 ** (-0.5)
norm_eps = 1e-06


def sent_to_all(shard, axis):
    devices = lax.axis_size(axis)
    return lax.all_to_all(
        jnp.broadcast_to(shard[None], (devices, *shard.shape)), axis, 0, 0, tiled=True
    )


def joined_along(blocks, dim):
    dims = list(blocks.shape[1:])
    dims[dim] *= blocks.shape[0]
    return jnp.moveaxis(blocks, 0, dim).reshape(dims)


def gather_directly(shard, axis, dim):
    blocks = sent_to_all(shard, axis)
    return joined_along(blocks, dim)


def shards(
    hidden,
    queries,
    latents,
    mem_latents,
    lengths,
    ids,
    gates,
    norm_gain,
    w_uv,
    w_out,
    w_gate,
    w_up,
    w_down,
):
    local_len = hidden.shape[1]
    seq_count = hidden.shape[2]
    model_width = hidden.shape[3]
    latent_dim = latents.shape[3]
    head_count = queries.shape[3] // latent_dim
    row_count = local_len * seq_count
    owner_count = lax.axis_size("expert")
    shard_index = lax.axis_index("expert")
    own_pos = shard_index * local_len + jnp.arange(local_len, dtype=jnp.int32)
    query_rows = queries[0].reshape(local_len, seq_count, head_count, latent_dim)
    memory = mem_latents[0]
    seq_limit = lengths[0]
    mem_scores = (
        jnp.einsum("tshl,msl->shtm", query_rows, memory, preferred_element_type=jnp.float32)
        * score_scale
    )
    first_max = jnp.max(mem_scores, axis=3)
    mem_weights = jnp.exp(mem_scores - first_max[..., None])
    first_sum = jnp.sum(mem_weights, axis=3)
    first_acc = jnp.einsum(
        "shtm,msl->tshl",
        mem_weights.astype(jnp.bfloat16),
        memory,
        preferred_element_type=jnp.float32,
    )

    def fold_step(carry, portion):
        old_max, old_sum, old_acc = carry
        key_rows = portion[0]
        key_pos = jnp.arange(key_rows.shape[0], dtype=jnp.int32)
        scores = (
            jnp.einsum("tshl,jsl->shtj", query_rows, key_rows, preferred_element_type=jnp.float32)
            * score_scale
        )
        causal = key_pos[None, :] <= own_pos[:, None]
        inside = key_pos[None, :] < seq_limit[:, None]
        visible = causal[None, None, :, :] & inside[:, None, None, :]
        scores = jnp.where(visible, scores, -jnp.inf)
        new_max = jnp.maximum(old_max, jnp.max(scores, axis=3))
        weights = jnp.exp(scores - new_max[..., None])
        factor = jnp.exp(old_max - new_max)
        new_sum = old_sum * factor + jnp.sum(weights, axis=3)
        contrib = jnp.einsum(
            "shtj,jsl->tshl",
            weights.astype(jnp.bfloat16),
            key_rows,
            preferred_element_type=jnp.float32,
        )
        new_acc = old_acc * jnp.transpose(factor, (2, 0, 1))[..., None] + contrib
        return (new_max, new_sum, new_acc)

    portion = lax.all_gather(latents, "expert", axis=1, tiled=True)
    last_pos = jnp.max(own_pos)
    final_max, final_sum, final_acc = lax.cond(
        jnp.int32(0) <= last_pos,
        lambda state: fold_step(state, portion),
        lambda state: state,
        (first_max, first_sum, first_acc),
    )
    attended = (final_acc / jnp.transpose(final_sum, (2, 0, 1))[..., None]).astype(jnp.bfloat16)
    values = jnp.einsum(
        "tshl,hlv->tshv",
        attended,
        gather_directly(w_uv, "dp", 0),
        preferred_element_type=jnp.float32,
    ).astype(jnp.bfloat16)
    flat_values = values.reshape(row_count, -1)
    attn_out = jnp.dot(
        flat_values,
        lax.all_gather(w_out, "dp", axis=0, tiled=True),
        preferred_element_type=jnp.float32,
    )
    residual = hidden[0].reshape(row_count, model_width).astype(jnp.float32) + attn_out
    mean_square = jnp.mean(residual * residual, axis=-1, keepdims=True)
    normed = (residual * lax.rsqrt(mean_square + norm_eps) * norm_gain.astype(jnp.float32)).astype(
        jnp.bfloat16
    )
    experts_here = w_gate.shape[0]
    expert_count = owner_count * experts_here
    top_count = ids.shape[3]
    capacity = min(row_count, row_count * top_count // expert_count + 2)
    flat_ids = ids[0].reshape(row_count * top_count)
    onehot = (flat_ids[:, None] == jnp.arange(expert_count, dtype=jnp.int32)[None, :]).astype(
        jnp.int32
    )
    before = jnp.cumsum(onehot, axis=0) - onehot
    slot_within = jnp.sum(before * onehot, axis=1)
    slot_index = (flat_ids * capacity + slot_within).reshape(row_count, top_count)
    matching = (
        jnp.arange(expert_count * capacity, dtype=jnp.int32)[:, None, None]
        == slot_index[None, :, :]
    )
    placing = jnp.any(matching, axis=2).astype(jnp.bfloat16)
    gate_rows = gates[0].reshape(row_count, top_count).astype(jnp.float32)
    mixing = jnp.sum(jnp.where(matching, gate_rows[None, :, :], jnp.float32(0.0)), axis=2).astype(
        jnp.bfloat16
    )
    outgoing = jnp.dot(placing, normed, preferred_element_type=jnp.float32).astype(jnp.bfloat16)
    outgoing = outgoing.reshape(owner_count, experts_here, capacity, model_width)
    incoming = lax.all_to_all(outgoing, "expert", split_axis=0, concat_axis=0, tiled=True)
    gate_h = jnp.einsum("necd,edf->necf", incoming, w_gate, preferred_element_type=jnp.float32)
    up_h = jnp.einsum("necd,edf->necf", incoming, w_up, preferred_element_type=jnp.float32)
    act = (jax.nn.silu(gate_h) * up_h).astype(jnp.bfloat16)
    produced = jnp.einsum("necf,efd->necd", act, w_down, preferred_element_type=jnp.float32).astype(
        jnp.bfloat16
    )
    returned = lax.all_to_all(produced, "expert", split_axis=0, concat_axis=0, tiled=True)
    combined_rows = returned.reshape(expert_count * capacity, model_width)
    routed = jnp.einsum("st,sd->td", mixing, combined_rows, preferred_element_type=jnp.float32)
    layer_out = (residual + routed).astype(jnp.bfloat16)
    return layer_out.reshape(1, local_len, seq_count, model_width)


def solution(mesh):
    return jax.shard_map(
        shards,
        mesh=mesh,
        in_specs=(
            P("dp", "expert", None, None),
            P("dp", "expert", None, None),
            P("dp", "expert", None, None),
            P("dp", None, None, None),
            P("dp", None),
            P("dp", "expert", None, None),
            P("dp", "expert", None, None),
            P(),
            P("dp", None, None),
            P("dp", None),
            P("expert", None, None),
            P("expert", None, None),
            P("expert", None, None),
        ),
        out_specs=P("dp", "expert", None, None),
        check_vma=False,
    )
```

profile of v0, /device:TPU:1, one launch (start us, length us, event | category | flops | bytes accessed | tf_op | source)
XLA Modules:
  0.0 415.4 jit_solution(3627106416608245663)
XLA Ops:
  6.5 1.7 copy.55
  9.0 2.1 broadcast_in_dim.29
  11.1 4.8 %all-to-all-start = ((bf16[4,2,512,128]{3,2,1,0:T(8,128)(2,1)}), bf16[4,2,512,128]{3,2,1,0:T(8,128)(2,1)}, u32[]{:S(2)}, u32[]{:S(2)}) async-start(bf16[4,2,512,128]{3,2,1,0:T(8,128)(2,1)} %broadcast_in_dim.29), calls=%async_computation | async-start | bytes 2097152 | tf_op jit(solution)/shard_map/all_to_all | solution.py:12
  16.4 2.6 reshape.151
  20.3 1.1 reshape.142
  21.5 1.8 reduce-window.6
  23.9 2.5 fusion.69
  26.7 2.7 convolution_bitcast_fusion
  29.9 67.4 %all-gather.3.cloned.1.call-done = bf16[1,4096,2,512]{3,1,2,0:T(8,128)(2,1)} async-done(((bf16[1,64,2,512]{3,1,2,0:T(8,128)(2,1)}), bf16[1,4096,2,512]{3,1,2,0:T(8,128)(2,1)}) %all-gather.3.cloned.1.call-update) | async-done | bytes 8388624 | tf_op jit(solution)/shard_map/all_gather | solution.py:94
  97.3 38.6 %conditional.1 = ((f32[2,8,64]{2,1,0:T(8,128)S(1)}, f32[64,2,8,512]{3,0,2,1:T(8,128)})) conditional(s32[]{:T(128)} %convert_element_type.74, (f32[2,8,64]{2,1,0:T(8,128)S(1)}, f32[64,2,8,512]{3,0,2,1:T(8,128)}) %tuple.12, (s32[64]{0:T(128)S(1)}, s32[1,2]{1,0:T(1,128)}, bf16[1,4096,2,512]{3,1,2,0:T(8,128)(2,1)}, bf16[64,2,8,512]{3,2,1,0:T(8,128)(2,1)}, ...), branch_computations={%region_3.0_spmd, %region_4.7_spmd} | conditional | flops 8637918208 | bytes 75047200 | solution.py:96
  97.5 0.7 iota_compare_fusion.1
  98.6 15.8 %fusion.2 = (f32[2,8,64]{2,1,0:T(8,128)}, f32[2,4096,64,8]{1,2,3,0:T(8,128)}) fusion(pred[2,64,4096]{2,1,0:T(8,128)(4,1)S(1)} %broadcast_and_fusion, bf16[64,2,8,512]{3,2,1,0:T(8,128)(2,1)} %get-tuple-element.57, bf16[1,4096,2,512]{3,1,2,0:T(8,128)(2,1)} %get-tuple-element.27), kind=kOutput, calls=%fused_computation.4 | convolution fusion | flops 4307549184 | bytes 26742784 | tf_op jit(solution)/shard_map/cond/branch_1_fun/tshl,jsl->shtj/dot_general | solution.py:74
  114.4 0.7 fusion.17
  115.1 12.4 %bitcast_add_fusion = f32[64,2,8,512]{3,0,2,1:T(8,128)} fusion(f32[64,2,8,512]{3,0,2,1:T(8,128)} %get-tuple-element.29, bf16[1,4096,2,512]{3,1,2,0:T(8,128)(2,1)} %get-tuple-element.27, f32[2,4096,64,8]{1,2,3,0:T(8,128)} %get-tuple-element.61, f32[2,8,64]{2,1,0:T(8,128)S(1)} %get-tuple-element.59, pred[2,64,4096]{2,1,0:T(8,128)(4,1)S(1)} %broadcast_and_fusion, ...), kind=kOutput, calls=%fused_computation.13 | convolution fusion | flops 4312793088 | bytes 29892608 | tf_op jit(solution)/shard_map/cond/branch_1_fun/shtj,jsl->tshl/dot_general | solution.py:85
  127.5 8.4 %fusion.1 = f32[2,8,64]{2,1,0:T(8,128)S(1)} fusion(f32[2,4096,64,8]{1,2,3,0:T(8,128)} %get-tuple-element.61, f32[2,8,64]{2,1,0:T(8,128)S(1)} %get-tuple-element.59, pred[2,64,4096]{2,1,0:T(8,128)(4,1)S(1)} %broadcast_and_fusion), kind=kLoop, calls=%fused_computation.3 | loop fusion | flops 16776192 | bytes 17309696 | tf_op jit(solution)/shard_map/cond/branch_1_fun/reduce_sum | solution.py:84
  135.9 2.4 fusion.48
  138.5 7.6 %all-gather.5.cloned.1.call-done = bf16[1024,2048]{1,0:T(8,128)(2,1)} async-done(((bf16[256,2048]{1,0:T(8,128)(2,1)}), bf16[1024,2048]{1,0:T(8,128)(2,1)}) %all-gather.5.cloned.1.call-update) | async-done | bytes 4194320 | tf_op jit(solution)/shard_map/all_gather | solution.py:112
  146.1 3.3 multiply_reduce_fusion
  149.4 1.0 copy-done.1
  150.4 3.0 convolution_convert_fusion
  153.4 6.0 %reshape.134 = bf16[64,1,14,2048]{3,2,0,1:T(8,128)(2,1)} reshape(bf16[896,2048]{1,0:T(8,128)(2,1)} %convolution_convert_fusion) | data formatting | bytes 7340032 | tf_op jit(solution)/shard_map/reshape | solution.py:141
  159.4 107.3 %all_to_all.15 = bf16[64,1,14,2048]{3,2,1,0:T(8,128)(2,1)S(1)} all-to-all(bf16[64,1,14,2048]{3,2,1,0:T(8,128)(2,1)} %bitcast.151), channel_id=1, replica_groups=mesh['dp'=4,'expert'=64] {'expert'}, dimensions={0} | all-to-all | bytes 7340032 | tf_op jit(solution)/shard_map/all_to_all | solution.py:142
  266.7 1.9 copy-done.2
  268.6 8.7 %fusion.22 = f32[64,14,704]{2,0,1:T(8,128)} fusion(bf16[64,1,14,2048]{3,2,1,0:T(8,128)(2,1)S(1)} %all_to_all.15, bf16[1,2048,704]{1,2,0:T(8,128)(2,1)S(1)} %copy-done.7), kind=kOutput, calls=%fused_computation.25 | convolution fusion | flops 2583691264 | bytes 9076736 | tf_op jit(solution)/shard_map/necd,edf->necf/dot_general | solution.py:143
  277.3 12.9 %convert_bitcast_fusion = bf16[64,1,14,2048]{3,0,2,1:T(8,128)(2,1)} fusion(bf16[1,704,2048]{2,1,0:T(8,128)(2,1)S(1)} %copy-done, bf16[1,2048,704]{1,2,0:T(8,128)(2,1)} %param.26, bf16[64,1,14,2048]{3,2,1,0:T(8,128)(2,1)} %copy-done.2, f32[64,14,704]{2,0,1:T(8,128)} %fusion.22), kind=kOutput, calls=%fused_computation.27 | convolution fusion | flops 5173002240 | bytes 15630336 | tf_op jit(solution)/shard_map/necf,efd->necd/dot_general | solution.py:146
  290.2 6.0 %copy.68 = bf16[64,1,14,2048]{3,2,1,0:T(8,128)(2,1)} copy(bf16[64,1,14,2048]{3,0,2,1:T(8,128)(2,1)} %convert_bitcast_fusion) | data formatting | bytes 7340032 | tf_op jit(solution)/shard_map/convert_element_type | solution.py:146
  296.2 6.2 %all-to-all-start.2 = ((bf16[64,1,14,2048]{3,2,1,0:T(8,128)(2,1)}), bf16[64,1,14,2048]{3,2,1,0:T(8,128)(2,1)}, u32[]{:S(2)}, u32[]{:S(2)}) async-start(bf16[64,1,14,2048]{3,2,1,0:T(8,128)(2,1)} %copy.68), calls=%async_computation.2 | async-start | bytes 8388608 | tf_op jit(solution)/shard_map/all_to_all | solution.py:149
  302.6 1.0 select_reduce_fusion
  303.6 94.6 %all-to-all-done.2 = bf16[64,1,14,2048]{3,2,1,0:T(8,128)(2,1)} async-done(((bf16[64,1,14,2048]{3,2,1,0:T(8,128)(2,1)}), bf16[64,1,14,2048]{3,2,1,0:T(8,128)(2,1)}, u32[]{:S(2)}, u32[]{:S(2)}) %all-to-all-start.2) | async-done | bytes 3670048 | tf_op jit(solution)/shard_map/all_to_all | solution.py:149
  398.3 6.0 %reshape.140 = bf16[896,2048]{1,0:T(8,128)(2,1)} reshape(bf16[64,1,14,2048]{3,2,1,0:T(8,128)(2,1)} %all-to-all-done.2) | data formatting | bytes 7340032 | tf_op jit(solution)/shard_map/reshape | solution.py:150
  404.2 3.1 fusion.34
  407.4 1.1 reshape.141
  (43 shorter events, 4.1 us)
Async XLA Ops:
  6.5 270.8 %copy-start = (bf16[1,704,2048]{2,1,0:T(8,128)(2,1)S(1)}, bf16[1,704,2048]{2,1,0:T(8,128)(2,1)}, u32[]{:S(2)}) copy-start(bf16[1,704,2048]{2,1,0:T(8,128)(2,1)} %param.27) | copy-start | bytes 8650756
  6.5 9.4 %copy-start.4 = (s32[1,64,2,6]{1,2,3,0:T(2,128)S(1)}, s32[1,64,2,6]{1,2,3,0:T(2,128)}, u32[]{:S(2)}) copy-start(s32[1,64,2,6]{1,2,3,0:T(2,128)} %param.20) | copy-start | bytes 9220
  6.5 13.8 %copy-start.3 = (bf16[1,64,2,2048]{3,2,1,0:T(2,128)(2,1)S(1)}, bf16[1,64,2,2048]{3,2,1,0:T(2,128)(2,1)}, u32[]{:S(2)}) copy-start(bf16[1,64,2,2048]{3,2,1,0:T(2,128)(2,1)} %param.15) | copy-start | bytes 1572868
  6.5 90.8 %all-gather.3.cloned.1.call-start = ((), (), s32[]{:S(2)}) async-start(), calls=%async_computation.3 | async-start | bytes 8519680 | tf_op jit(solution)/shard_map/all_gather | solution.py:94
  8.3 137.8 %all-gather.5.cloned.1.call-start = ((), (), s32[]{:S(2)}) async-start(), calls=%async_computation.4 | async-start | bytes 5242880 | tf_op jit(solution)/shard_map/all_gather | solution.py:112
  11.1 124.8 %all-to-all-start = ((bf16[4,2,512,128]{3,2,1,0:T(8,128)(2,1)}), bf16[4,2,512,128]{3,2,1,0:T(8,128)(2,1)}, u32[]{:S(2)}, u32[]{:S(2)}) async-start(bf16[4,2,512,128]{3,2,1,0:T(8,128)(2,1)} %broadcast_in_dim.29), calls=%async_computation | async-start | bytes 2097152 | tf_op jit(solution)/shard_map/all_to_all | solution.py:12
  16.0 10.7 %copy-start.5 = (bf16[2048]{0:T(1024)(128)(2,1)S(1)}, bf16[2048]{0:T(1024)(128)(2,1)}, u32[]{:S(2)}) copy-start(bf16[2048]{0:T(1024)(128)(2,1)} %param.22) | copy-start | bytes 12292
  149.4 1.0 copy-start.1
  159.4 109.2 %copy-start.7 = (bf16[1,2048,704]{1,2,0:T(8,128)(2,1)S(1)}, bf16[1,2048,704]{1,2,0:T(8,128)(2,1)}, u32[]{:S(2)}) copy-start(bf16[1,2048,704]{1,2,0:T(8,128)(2,1)} %param.25) | copy-start | bytes 8650756
  266.7 1.9 copy-start.2
  296.2 6.2 %copy-start.6 = (bf16[1,64,2,6]{1,2,3,0:T(2,128)(2,1)S(1)}, bf16[1,64,2,6]{1,2,3,0:T(2,128)(2,1)}, u32[]{:S(2)}) copy-start(bf16[1,64,2,6]{1,2,3,0:T(2,128)(2,1)} %param.21) | copy-start | bytes 4612
  296.2 102.0 %all-to-all-start.2 = ((bf16[64,1,14,2048]{3,2,1,0:T(8,128)(2,1)}), bf16[64,1,14,2048]{3,2,1,0:T(8,128)(2,1)}, u32[]{:S(2)}, u32[]{:S(2)}) async-start(bf16[64,1,14,2048]{3,2,1,0:T(8,128)(2,1)} %copy.68), calls=%async_computation.2 | async-start | bytes 8388608 | tf_op jit(solution)/shard_map/all_to_all | solution.py:149
Sparse Core Ops, SparseCore 0:
  10.1 87.1 all-gather.2
  99.1 46.9 all-gather.4
where the time goes:
time: 416 us; the launch traced here: 415 us
  waiting for transfers between devices  170 us (41%)
  blocking collectives  107 us (26%)
  matrix products  66.9 us (16%)
  local copies, waits for them, and re-layouts  30.9 us (7%)
  other arithmetic  14.6 us (4%)
  between operations  14.2 us (3%)
  starting transfers between devices  11.1 us (3%)
    all_to_all x1, blocking collectives, shards(): lax.all_to_all(outgoing, 'expert', split_axis=0, concat_axis=0, tiled=True)  107 us
    all_to_all x1, waiting for transfers between devices, shards(): lax.all_to_all(produced, 'expert', split_axis=0, concat_axis=0, tiled=True)  94.6 us
    all_gather x1, waiting for transfers between devices, shards(): portion = lax.all_gather(latents, 'expert', axis=1, tiled=True)  67.4 us
    dot_general x1, matrix products, fold_step(): jnp.einsum('tshl,jsl->shtj', query_rows, key_rows, preferred_element_type...  15.8 us
    dot_general x1, matrix products, shards(): jnp.einsum('necf,efd->necd', act, w_down, preferred_element_type=jnp.floa...  12.9 us
    dot_general x1, matrix products, fold_step(): jnp.einsum('shtj,jsl->tshl', weights.astype(jnp.bfloat16), key_rows, pref...  12.4 us
    dot_general x1, matrix products, shards(): jnp.einsum('necd,edf->necf', incoming, w_gate, preferred_element_type=jnp...  8.67 us
    reduce_sum x1, other arithmetic, fold_step(): new_sum = old_sum * factor + jnp.sum(weights, axis=3)  8.39 us
  transfers between devices with their start and end apart: 4, of which 3 were waited for; matrix products, arithmetic and copies ran while one was open for 14% of the time, Pallas kernels for 0%

commit v1 on v0

--- a/solution.py
+++ b/solution.py
@@ -91,7 +91,7 @@
         new_acc = old_acc * jnp.transpose(factor, (2, 0, 1))[..., None] + contrib
         return (new_max, new_sum, new_acc)
 
-    portion = lax.all_gather(latents, "expert", axis=1, tiled=True)
+    portion = jnp.concatenate(lax.all_gather(latents, "expert"), axis=1)
     last_pos = jnp.max(own_pos)
     final_max, final_sum, final_acc = lax.cond(
         jnp.int32(0) <= last_pos,

time: 416 us -> 416 us (level)
  transfers between devices with their start and end apart: 4 -> 4, of which waited for: 3 -> 3; matrix products, arithmetic and copies ran while one was open for 14% -> 13% of each run, Pallas kernels for 0% -> 0%
where the time goes in v1:
time: 416 us; the launch traced here: 415 us
  waiting for transfers between devices  172 us (41%)
  blocking collectives  107 us (26%)
  matrix products  62.8 us (15%)
  local copies, waits for them, and re-layouts  32.3 us (8%)
  other arithmetic  15.4 us (4%)
  between operations  14.2 us (3%)
  starting transfers between devices  11.1 us (3%)
    all_to_all x1, blocking collectives, shards(): lax.all_to_all(outgoing, 'expert', split_axis=0, concat_axis=0, tiled=True)  107 us
    all_to_all x1, waiting for transfers between devices, shards(): lax.all_to_all(produced, 'expert', split_axis=0, concat_axis=0, tiled=True)  94.6 us
    all_gather x1, waiting for transfers between devices, shards(): portion = jnp.concatenate(lax.all_gather(latents, 'expert'), axis=1)  67.4 us
    dot_general x1, matrix products, fold_step(): jnp.einsum('tshl,jsl->shtj', query_rows, key_rows, preferred_element_type...  15.8 us
    dot_general x1, matrix products, shards(): jnp.einsum('necf,efd->necd', act, w_down, preferred_element_type=jnp.floa...  12.9 us
    all_gather x1, waiting for transfers between devices, shards(): lax.all_gather(w_out, 'dp', axis=0, tiled=True)  9.5 us
    reduce_sum x1, other arithmetic, fold_step(): new_sum = old_sum * factor + jnp.sum(weights, axis=3)  9.16 us
    dot_general x1, matrix products, shards(): jnp.einsum('necd,edf->necf', incoming, w_gate, preferred_element_type=jnp...  8.67 us
  transfers between devices with their start and end apart: 4, of which 3 were waited for; matrix products, arithmetic and copies ran while one was open for 13% of the time, Pallas kernels for 0%

profile of v1, /device:TPU:1, one launch (start us, length us, event | category | flops | bytes accessed | tf_op | source)
XLA Modules:
  0.0 415.4 jit_solution(4709314118830544687)
XLA Ops:
  6.5 1.7 copy.55
  9.0 2.1 broadcast_in_dim.29
  11.1 4.8 %all-to-all-start = ((bf16[4,2,512,128]{3,2,1,0:T(8,128)(2,1)}), bf16[4,2,512,128]{3,2,1,0:T(8,128)(2,1)}, u32[]{:S(2)}, u32[]{:S(2)}) async-start(bf16[4,2,512,128]{3,2,1,0:T(8,128)(2,1)} %broadcast_in_dim.29), calls=%async_computation | async-start | bytes 2097152 | tf_op jit(solution)/shard_map/all_to_all | solution.py:12
  16.4 2.6 reshape.152
  20.3 1.1 reshape.142
  21.5 1.8 reduce-window.6
  23.9 2.5 fusion.65
  26.7 2.7 convolution_bitcast_fusion
  29.9 67.4 %all-gather.6.cloned.1.call-done = bf16[64,64,2,512]{3,1,0,2:T(8,128)(2,1)} async-done(((bf16[1,64,2,512]{3,1,0,2:T(8,128)(2,1)}), bf16[64,64,2,512]{3,1,0,2:T(8,128)(2,1)}) %all-gather.6.cloned.1.call-update) | async-done | bytes 8388624 | tf_op jit(solution)/shard_map/all_gather | solution.py:94
  97.3 36.7 %conditional.1 = ((f32[2,8,64]{2,1,0:T(8,128)S(1)}, f32[64,2,8,512]{3,0,2,1:T(8,128)})) conditional(s32[]{:T(128)} %convert_element_type.74, (f32[2,8,64]{2,1,0:T(8,128)S(1)}, f32[64,2,8,512]{3,0,2,1:T(8,128)}) %tuple.12, (s32[64]{0:T(128)S(1)}, s32[1,2]{1,0:T(1,128)}, bf16[64,1,64,2,512]{4,2,0,3,1:T(8,128)(2,1)}, bf16[64,2,8,512]{3,2,1,0:T(8,128)(2,1)}, ...), branch_computations={%region_3.0_spmd, %region_4.7_spmd} | conditional | flops 8637918208 | bytes 125378928 | solution.py:96
  97.5 0.7 iota_compare_fusion.1
  98.6 15.8 %fusion.2 = (f32[2,8,64]{2,1,0:T(8,128)}, f32[2,4096,64,8]{1,2,3,0:T(8,128)}) fusion(pred[2,64,4096]{2,1,0:T(8,128)(4,1)S(1)} %broadcast_and_fusion, bf16[4096,2,512,1]{2,0,3,1:T(8,128)(2,1)} %bitcast.157, bf16[64,2,8,512]{3,2,1,0:T(8,128)(2,1)} %get-tuple-element.57), kind=kOutput, calls=%fused_computation.4 | convolution fusion | flops 4307549184 | bytes 26742784 | tf_op jit(solution)/shard_map/cond/branch_1_fun/tshl,jsl->shtj/dot_general | solution.py:74
  115.1 9.2 %fusion.1 = f32[2,8,64]{2,1,0:T(8,128)S(1)} fusion(f32[2,4096,64,8]{1,2,3,0:T(8,128)} %get-tuple-element.61, f32[2,8,64]{2,1,0:T(8,128)S(1)} %get-tuple-element.59, pred[2,64,4096]{2,1,0:T(8,128)(4,1)S(1)} %broadcast_and_fusion), kind=kLoop, calls=%fused_computation.3 | loop fusion | flops 16776192 | bytes 17309696 | tf_op jit(solution)/shard_map/cond/branch_1_fun/reduce_sum | solution.py:84
  124.3 8.4 %bitcast_add_fusion = f32[64,2,8,512]{3,0,2,1:T(8,128)S(1)} fusion(f32[64,2,8,512]{3,0,2,1:T(8,128)S(1)} %copy-done.3, bf16[4096,2,512,1]{2,0,3,1:T(8,128)(2,1)S(1)} %bitcast.158, f32[2,4096,64,8]{1,2,3,0:T(8,128)} %get-tuple-element.61, f32[2,8,64]{2,1,0:T(8,128)S(1)} %get-tuple-element.59, pred[2,64,4096]{2,1,0:T(8,128)(4,1)S(1)} %broadcast_and_fusion, ...), kind=kOutput, calls=%fused_computation.10 | convolution fusion | flops 4312793088 | bytes 29892608 | tf_op jit(solution)/shard_map/cond/branch_1_fun/shtj,jsl->tshl/dot_general | solution.py:85
  132.7 1.3 copy-done.4
  134.0 2.4 fusion.44
  136.6 9.5 %all-gather.4.cloned.1.call-done = bf16[1024,2048]{1,0:T(8,128)(2,1)} async-done(((bf16[256,2048]{1,0:T(8,128)(2,1)}), bf16[1024,2048]{1,0:T(8,128)(2,1)}) %all-gather.4.cloned.1.call-update) | async-done | bytes 4194320 | tf_op jit(solution)/shard_map/all_gather | solution.py:112
  146.1 3.3 multiply_reduce_fusion
  149.4 1.0 copy-done.1
  150.4 3.0 convolution_convert_fusion
  153.4 6.0 %reshape.134 = bf16[64,1,14,2048]{3,2,0,1:T(8,128)(2,1)} reshape(bf16[896,2048]{1,0:T(8,128)(2,1)} %convolution_convert_fusion) | data formatting | bytes 7340032 | tf_op jit(solution)/shard_map/reshape | solution.py:141
  159.4 107.3 %all_to_all.15 = bf16[64,1,14,2048]{3,2,1,0:T(8,128)(2,1)S(1)} all-to-all(bf16[64,1,14,2048]{3,2,1,0:T(8,128)(2,1)} %bitcast.147), channel_id=1, replica_groups=mesh['dp'=4,'expert'=64] {'expert'}, dimensions={0} | all-to-all | bytes 7340032 | tf_op jit(solution)/shard_map/all_to_all | solution.py:142
  266.7 1.9 copy-done.2
  268.6 8.7 %fusion.18 = f32[64,14,704]{2,0,1:T(8,128)} fusion(bf16[64,1,14,2048]{3,2,1,0:T(8,128)(2,1)S(1)} %all_to_all.15, bf16[1,2048,704]{1,2,0:T(8,128)(2,1)S(1)} %copy-done.10), kind=kOutput, calls=%fused_computation.23 | convolution fusion | flops 2583691264 | bytes 9076736 | tf_op jit(solution)/shard_map/necd,edf->necf/dot_general | solution.py:143
  277.3 12.9 %convert_bitcast_fusion = bf16[64,1,14,2048]{3,0,2,1:T(8,128)(2,1)} fusion(bf16[1,704,2048]{2,1,0:T(8,128)(2,1)S(1)} %copy-done, bf16[1,2048,704]{1,2,0:T(8,128)(2,1)} %param.26, bf16[64,1,14,2048]{3,2,1,0:T(8,128)(2,1)} %copy-done.2, f32[64,14,704]{2,0,1:T(8,128)} %fusion.18), kind=kOutput, calls=%fused_computation.25 | convolution fusion | flops 5173002240 | bytes 15630336 | tf_op jit(solution)/shard_map/necf,efd->necd/dot_general | solution.py:146
  290.2 6.0 %copy.68 = bf16[64,1,14,2048]{3,2,1,0:T(8,128)(2,1)} copy(bf16[64,1,14,2048]{3,0,2,1:T(8,128)(2,1)} %convert_bitcast_fusion) | data formatting | bytes 7340032 | tf_op jit(solution)/shard_map/convert_element_type | solution.py:146
  296.2 6.2 %all-to-all-start.2 = ((bf16[64,1,14,2048]{3,2,1,0:T(8,128)(2,1)}), bf16[64,1,14,2048]{3,2,1,0:T(8,128)(2,1)}, u32[]{:S(2)}, u32[]{:S(2)}) async-start(bf16[64,1,14,2048]{3,2,1,0:T(8,128)(2,1)} %copy.68), calls=%async_computation.2 | async-start | bytes 8388608 | tf_op jit(solution)/shard_map/all_to_all | solution.py:149
  302.6 1.0 select_reduce_fusion
  303.6 94.6 %all-to-all-done.2 = bf16[64,1,14,2048]{3,2,1,0:T(8,128)(2,1)} async-done(((bf16[64,1,14,2048]{3,2,1,0:T(8,128)(2,1)}), bf16[64,1,14,2048]{3,2,1,0:T(8,128)(2,1)}, u32[]{:S(2)}, u32[]{:S(2)}) %all-to-all-start.2) | async-done | bytes 3670048 | tf_op jit(solution)/shard_map/all_to_all | solution.py:149
  398.3 6.0 %reshape.140 = bf16[896,2048]{1,0:T(8,128)(2,1)} reshape(bf16[64,1,14,2048]{3,2,1,0:T(8,128)(2,1)} %all-to-all-done.2) | data formatting | bytes 7340032 | tf_op jit(solution)/shard_map/reshape | solution.py:150
  404.2 3.1 fusion.30
  407.4 1.1 reshape.141
  (49 shorter events, 4.8 us)
Async XLA Ops:
  6.5 270.8 %copy-start = (bf16[1,704,2048]{2,1,0:T(8,128)(2,1)S(1)}, bf16[1,704,2048]{2,1,0:T(8,128)(2,1)}, u32[]{:S(2)}) copy-start(bf16[1,704,2048]{2,1,0:T(8,128)(2,1)} %param.27) | copy-start | bytes 8650756
  6.5 9.4 %copy-start.6 = (s32[1,64,2,6]{1,2,3,0:T(2,128)S(1)}, s32[1,64,2,6]{1,2,3,0:T(2,128)}, u32[]{:S(2)}) copy-start(s32[1,64,2,6]{1,2,3,0:T(2,128)} %param.20) | copy-start | bytes 9220
  6.5 13.8 %copy-start.5 = (bf16[1,64,2,2048]{3,2,1,0:T(2,128)(2,1)S(1)}, bf16[1,64,2,2048]{3,2,1,0:T(2,128)(2,1)}, u32[]{:S(2)}) copy-start(bf16[1,64,2,2048]{3,2,1,0:T(2,128)(2,1)} %param.15) | copy-start | bytes 1572868
  6.5 90.8 %all-gather.6.cloned.1.call-start = ((), (), s32[]{:S(2)}) async-start(), calls=%async_computation.4 | async-start | bytes 8519680 | tf_op jit(solution)/shard_map/all_gather | solution.py:94
  8.3 137.8 %all-gather.4.cloned.1.call-start = ((), (), s32[]{:S(2)}) async-start(), calls=%async_computation.3 | async-start | bytes 5242880 | tf_op jit(solution)/shard_map/all_gather | solution.py:112
  11.1 122.9 %all-to-all-start = ((bf16[4,2,512,128]{3,2,1,0:T(8,128)(2,1)}), bf16[4,2,512,128]{3,2,1,0:T(8,128)(2,1)}, u32[]{:S(2)}, u32[]{:S(2)}) async-start(bf16[4,2,512,128]{3,2,1,0:T(8,128)(2,1)} %broadcast_in_dim.29), calls=%async_computation | async-start | bytes 2097152 | tf_op jit(solution)/shard_map/all_to_all | solution.py:12
  16.0 10.7 %copy-start.7 = (bf16[2048]{0:T(1024)(128)(2,1)S(1)}, bf16[2048]{0:T(1024)(128)(2,1)}, u32[]{:S(2)}) copy-start(bf16[2048]{0:T(1024)(128)(2,1)} %param.22) | copy-start | bytes 12292
  115.1 9.2 %copy-start.3 = (f32[64,2,8,512]{3,0,2,1:T(8,128)S(1)}, f32[64,2,8,512]{3,0,2,1:T(8,128)}, u32[]{:S(2)}) copy-start(f32[64,2,8,512]{3,0,2,1:T(8,128)} %get-tuple-element.29) | copy-start | bytes 6291460 | tf_op jit(solution)/shard_map/cond
  115.1 9.2 %copy-start.9 = (bf16[64,1,64,2,512]{4,2,0,3,1:T(8,128)(2,1)S(1)}, bf16[64,1,64,2,512]{4,2,0,3,1:T(8,128)(2,1)}, u32[]{:S(2)}) copy-start(bf16[64,1,64,2,512]{4,2,0,3,1:T(8,128)(2,1)} %get-tuple-element.27) | copy-start | bytes 25165828 | tf_op jit(solution)/shard_map/cond
  132.7 1.4 copy-start.4
  149.4 1.0 copy-start.1
  159.4 109.2 %copy-start.10 = (bf16[1,2048,704]{1,2,0:T(8,128)(2,1)S(1)}, bf16[1,2048,704]{1,2,0:T(8,128)(2,1)}, u32[]{:S(2)}) copy-start(bf16[1,2048,704]{1,2,0:T(8,128)(2,1)} %param.25) | copy-start | bytes 8650756
  266.7 1.9 copy-start.2
  296.2 6.2 %copy-start.8 = (bf16[1,64,2,6]{1,2,3,0:T(2,128)(2,1)S(1)}, bf16[1,64,2,6]{1,2,3,0:T(2,128)(2,1)}, u32[]{:S(2)}) copy-start(bf16[1,64,2,6]{1,2,3,0:T(2,128)(2,1)} %param.21) | copy-start | bytes 4612
  296.2 102.0 %all-to-all-start.2 = ((bf16[64,1,14,2048]{3,2,1,0:T(8,128)(2,1)}), bf16[64,1,14,2048]{3,2,1,0:T(8,128)(2,1)}, u32[]{:S(2)}, u32[]{:S(2)}) async-start(bf16[64,1,14,2048]{3,2,1,0:T(8,128)(2,1)} %copy.68), calls=%async_computation.2 | async-start | bytes 8388608 | tf_op jit(solution)/shard_map/all_to_all | solution.py:149
Sparse Core Ops, SparseCore 0:
  10.1 87.1 all-gather.5
  99.1 46.9 all-gather.3
